TPU v7x, 128 devices: a whole 4x4x4 slice. The times are simulated.
128 devices in a mesh: rep: 8 (over y, x_hi), tp: 16 (over x_lo, z, core).
Axes of the slice: x: 4 (x_hi: 2, x_lo: 2; x = x_hi * 2 + x_lo), y: 4, z: 4, core: 2. Of those that a mesh axis runs over, the one named last changes fastest.
Arguments:
- hidden: bfloat16 [4096, 14336], P('rep'), may hold values from -6 to 6
- ln_gain: float32 [14336], replicated, may hold values from 0.1 to 1.9
- ln_shift: float32 [14336], replicated, may hold values from -3 to 3
- qkv_weight: bfloat16 [14336, 32, 384], P(('rep', 'tp')), may hold values from -0.046875 to 0.046875
- qkv_bias: float32 [32, 384], P('tp'), may hold values from -64 to 64
- out_weight: bfloat16 [14336, 32, 128], P('tp'), may hold values from -0.375 to 0.375
- out_bias: float32 [14336], P('tp'), may hold values from -3 to 3
- slope_index: int32 [32], P('tp'), may hold values from 0 to 111
Outputs:
- attended: bfloat16 [4096, 14336], P('rep', 'tp')
All inputs are finite; a program needn't handle non-finite values.
Results may differ from a plain program's by a relative error of at most 0.024.
The roundings to bfloat16 on the way count: a program that leaves them out, or rounds other values in their place, can miss the bound.
Values may be sent and summed in bfloat16 or wider, within the bound.
A program may use at most 192 MiB of HBM per device.

v0:
```python
import math
import jax
import jax.numpy as jnp
from jax import lax
from jax.sharding import PartitionSpec as P

N_SLOPES = 112
epsilon = 1e-05


def slope_values(slope_index):
    power = 1 << N_SLOPES.bit_length() - 1
    index_float = slope_index.astype(jnp.float32)
    leading = jnp.exp2(-8.0 * (index_float + 1.0) / power)
    between = jnp.exp2(-4.0 * (2.0 * (index_float - power) + 1.0) / power)
    return jnp.where(slope_index < power, leading, between)


def layer_norm(hidden, ln_gain, ln_shift):
    inputs_f32 = hidden.astype(jnp.float32)
    average = jnp.mean(inputs_f32, axis=-1, keepdims=True)
    centred = inputs_f32 - average
    variance = jnp.mean(centred * centred, axis=-1, keepdims=True)
    return (centred * lax.rsqrt(variance + epsilon) * ln_gain + ln_shift).astype(jnp.bfloat16)


def shards(hidden, ln_gain, ln_shift, qkv_weight, qkv_bias, out_weight, out_bias, slope_index):
    seq_rows = hidden.shape[0]
    heads_here = qkv_bias.shape[0]
    head_size = qkv_bias.shape[1] // 3
    flat_width = heads_here * 3 * head_size
    normed = layer_norm(hidden, ln_gain, ln_shift)
    regrouped = lax.all_to_all(qkv_weight, "tp", split_axis=1, concat_axis=0, tiled=True)
    weight_piece = lax.all_gather(regrouped, "rep", axis=0, tiled=True)
    flat_piece = weight_piece.reshape(weight_piece.shape[0], flat_width)
    projected = jnp.dot(normed, flat_piece, preferred_element_type=jnp.float32)
    qkv = (projected.reshape(seq_rows, heads_here, 3 * head_size) + qkv_bias).astype(jnp.bfloat16)
    query = qkv[:, :, :head_size]
    keys = qkv[:, :, head_size : 2 * head_size]
    values = qkv[:, :, 2 * head_size :]
    slopes = slope_values(slope_index)
    scores = jnp.einsum(
        "sha,tha->hst", query, keys, preferred_element_type=jnp.float32
    ) / math.sqrt(head_size)
    position = lax.iota(jnp.int32, seq_rows)
    distance = (position[:, None] - position[None, :]).astype(jnp.float32)
    scores = scores - slopes[:, None, None] * distance
    scores = jnp.where(distance >= 0.0, scores, -1e30)
    highest = jnp.max(scores, axis=-1, keepdims=True)
    powered = jnp.exp(scores - highest)
    attention = (powered / jnp.sum(powered, axis=-1, keepdims=True)).astype(jnp.bfloat16)
    context = jnp.einsum(
        "hst,tha->sha", attention, values, preferred_element_type=jnp.float32
    ).astype(jnp.bfloat16)
    context = context.reshape(seq_rows, heads_here * head_size)
    everything = lax.all_gather(context, "tp", axis=1, tiled=True)
    groups = lax.axis_size("tp")
    group_width = heads_here * head_size
    context_blocks = everything.reshape(seq_rows, groups, group_width)
    weight_blocks = out_weight.reshape(out_weight.shape[0], groups, group_width)
    partials = jnp.einsum(
        "sgk,dgk->gsd", context_blocks, weight_blocks, preferred_element_type=jnp.float32
    ).astype(jnp.bfloat16)
    partials = lax.optimization_barrier(partials)
    result = jnp.sum(partials.astype(jnp.float32), axis=0) + out_bias
    return result.astype(jnp.bfloat16)


def solution(mesh):
    return jax.shard_map(
        shards,
        mesh=mesh,
        in_specs=(
            P("rep", None),
            P(),
            P(),
            P(("rep", "tp"), None, None),
            P("tp", None),
            P("tp", None, None),
            P("tp"),
            P("tp"),
        ),
        out_specs=P("rep", "tp"),
        check_vma=False,
    )
```

profile of v0, /device:TPU:1, one launch (start us, length us, event | category | flops | bytes accessed | tf_op | source)
XLA Modules:
  0.0 399.7 jit_solution(10070072146498777757)
XLA Ops:
  6.5 2.8 copy.16
  9.3 41.7 %all_to_all.18 = bf16[112,32,384]{2,0,1:T(8,128)(2,1)S(1)} all-to-all(bf16[112,32,384]{2,0,1:T(8,128)(2,1)S(1)} %copy.16), channel_id=1, replica_groups=mesh['rep'=8,'tp'=16] {'tp'}, dimensions={1} | all-to-all | bytes 5505024 | tf_op jit(solution)/shard_map/all_to_all | solution.py:33
  51.0 1.8 copy.17
  52.8 0.0 all-gather.3.cloned.1.call-update
  52.9 0.0 all-gather.5.cloned.1.call-start
  52.9 0.2 broadcast_compare_fusion
  53.1 0.1 subtract_convert_fusion
  53.3 0.2 copy-done.5
  53.5 7.2 %convert_reduce_fusion = f32[512]{0:T(512)S(1)} fusion(bf16[512,14336]{1,0:T(8,128)(2,1)} %param.8), kind=kLoop, calls=%fused_computation.2 | loop fusion | flops 14679552 | bytes 14682112 | tf_op jit(solution)/shard_map/reduce_sum | solution.py:21
  60.7 11.6 %fusion.3 = f32[512]{0:T(512)S(1)} fusion(bf16[512,14336]{1,0:T(8,128)(2,1)} %param.8, f32[512]{0:T(512)S(1)} %broadcast_multiply_fusion), kind=kLoop, calls=%fused_computation.5 | loop fusion | flops 29359616 | bytes 14684160 | tf_op jit(solution)/shard_map/reduce_sum | solution.py:23
  72.3 0.0 copy-start.4
  72.3 208.5 %all-gather.3.cloned.1.call-done = bf16[14336,2,384]{2,0,1:T(8,128)(2,1)} async-done(((bf16[1792,2,384]{2,0,1:T(8,128)(2,1)}), bf16[14336,2,384]{2,0,1:T(8,128)(2,1)}) %all-gather.3.cloned.1.call-update) | async-done | bytes 22020112 | tf_op jit(solution)/shard_map/all_gather | solution.py:34
  280.8 26.1 %copy.18 = bf16[14336,2,384]{0,2,1:T(8,128)(2,1)} copy(bf16[14336,2,384]{2,0,1:T(8,128)(2,1)} %all-gather.3.cloned.1.call-done) | data formatting | bytes 44040192 | tf_op jit(solution)/shard_map/all_gather | solution.py:34
  306.9 17.8 %add_convert_fusion.1 = bf16[512,2,384]{2,0,1:T(8,128)(2,1)S(1)} fusion(bf16[14336,2,384]{0,2,1:T(8,128)(2,1)} %copy.18, bf16[512,14336]{1,0:T(8,128)(2,1)} %param.8, f32[14336]{0:T(1024)S(1)} %copy-done.2, f32[14336]{0:T(1024)S(1)} %copy-done.3, f32[512]{0:T(512)S(1)} %add_rsqrt_fusion, f32[512]{0:T(512)S(1)} %broadcast_multiply_fusion, ...), kind=kOutput, calls=%fused_computation.23 | convolution fusion | flops 11319115776 | bytes 37608448 | tf_op jit(solution)/shard_map/dot_general | solution.py:36
  324.7 0.9 copy-done
  325.6 0.6 subtract_select_fusion
  326.2 2.0 fusion.30
  328.2 2.3 convolution_convert_fusion.1
  330.5 0.0 all-gather.5.cloned.1.call-update
  330.6 11.5 %reshape.49 = bf16[896,16,256]{2,1,0:T(8,128)(2,1)} reshape(bf16[896,32,128]{2,1,0:T(8,128)(2,1)} %param.13) | data formatting | bytes 14680064 | tf_op jit(solution)/shard_map/reshape | solution.py:60
  342.0 25.0 %all-gather.5.cloned.1.call-done = bf16[512,4096]{0,1:T(8,128)(2,1)} async-done(((bf16[512,256]{0,1:T(8,128)(2,1)}), bf16[512,4096]{0,1:T(8,128)(2,1)}) %all-gather.5.cloned.1.call-update) | async-done | bytes 4194320 | tf_op jit(solution)/shard_map/all_gather | solution.py:56
  367.0 17.4 %convolution_convert_fusion = bf16[16,512,896]{2,1,0:T(8,128)(2,1)} fusion(bf16[512,16,256]{0,2,1:T(8,128)(2,1)} %bitcast.26, bf16[896,16,256]{2,1,0:T(8,128)(2,1)} %reshape.49), kind=kOutput, calls=%fused_computation.17 | convolution fusion | flops 3765436416 | bytes 26214400 | tf_op jit(solution)/shard_map/sgk,dgk->gsd/dot_general | solution.py:61
  384.4 7.4 %convert_reduce_fusion.1 = f32[512,896]{1,0:T(8,128)S(1)} fusion(bf16[16,512,896]{2,1,0:T(8,128)(2,1)} %convolution_convert_fusion), kind=kLoop, calls=%fused_computation.9 | loop fusion | flops 14221312 | bytes 16515072 | tf_op jit(solution)/shard_map/reduce_sum | solution.py:65
  391.8 1.0 add_convert_fusion
  (13 shorter events, 0.1 us)
Async XLA Ops:
  6.5 274.3 %all-gather.3.cloned.1.call-start = ((), (), s32[]{:S(2)}) async-start(), calls=%async_computation.1 | async-start | bytes 24772608 | tf_op jit(solution)/shard_map/all_gather | solution.py:34
  52.8 0.7 copy-start.5
  52.9 314.2 %all-gather.5.cloned.1.call-start = ((), (), s32[]{:S(2)}) async-start(), calls=%async_computation.2 | async-start | bytes 4456448 | tf_op jit(solution)/shard_map/all_gather | solution.py:56
  72.3 234.6 %copy-start.2 = (f32[14336]{0:T(1024)S(1)}, f32[14336]{0:T(1024)}, u32[]{:S(2)}) copy-start(f32[14336]{0:T(1024)} %param.10) | copy-start | bytes 172036
  72.3 234.6 %copy-start.3 = (f32[14336]{0:T(1024)S(1)}, f32[14336]{0:T(1024)}, u32[]{:S(2)}) copy-start(f32[14336]{0:T(1024)} %param.9) | copy-start | bytes 172036
  72.3 234.6 %copy-start.4 = (f32[2,384]{1,0:T(2,128)S(1)}, f32[2,384]{1,0:T(2,128)}, u32[]{:S(2)}) copy-start(f32[2,384]{1,0:T(2,128)} %param.12) | copy-start | bytes 9220
  324.7 0.9 copy-start
  384.4 7.4 %copy-start.1 = (f32[896]{0:T(1024)S(1)}, f32[896]{0:T(1024)}, u32[]{:S(2)}) copy-start(f32[896]{0:T(1024)} %param.14) | copy-start | bytes 10756
Sparse Core Ops, SparseCore 0:
  53.0 227.7 all-gather.2
  330.7 36.3 all-gather.4
where the time goes:
time: 401 us; the launch traced here: 400 us
  waiting for transfers between devices  233 us (58%)
  local copies, waits for them, and re-layouts  43.3 us (11%)
  blocking collectives  41.7 us (10%)
  matrix products  40.1 us (10%)
  other arithmetic  27.6 us (7%)
  between operations  13.5 us (3%)
    all_gather x1, waiting for transfers between devices, shards(): weight_piece = lax.all_gather(regrouped, 'rep', axis=0, tiled=True)  208 us
    all_to_all x1, blocking collectives, shards(): lax.all_to_all(qkv_weight, 'tp', split_axis=1, concat_axis=0, tiled=True)  41.7 us
    all_gather x1, local copies, waits for them, and re-layouts, shards(): weight_piece = lax.all_gather(regrouped, 'rep', axis=0, tiled=True)  26.1 us
    all_gather x1, waiting for transfers between devices, shards(): everything = lax.all_gather(context, 'tp', axis=1, tiled=True)  25 us
    dot_general x1, matrix products, shards(): projected = jnp.dot(normed, flat_piece, preferred_element_type=jnp.float32)  17.8 us
    dot_general x1, matrix products, shards(): jnp.einsum('sgk,dgk->gsd', context_blocks, weight_blocks, preferred_eleme...  17.4 us
    reduce_sum x1, other arithmetic, layer_norm(): variance = jnp.mean(centred * centred, axis=-1, keepdims=True)  11.6 us
    reshape x1, local copies, waits for them, and re-layouts, shards(): weight_blocks = out_weight.reshape(out_weight.shape[0], groups, group_width)  11.5 us
  transfers between devices with their start and end apart: 2, of which 2 were waited for; matrix products, arithmetic and copies ran while one was open for 8% of the time, Pallas kernels for 0%

commit v1 on v0

--- a/solution.py
+++ b/solution.py
@@ -1,3 +1,4 @@
+import functools
 import math
 import jax
 import jax.numpy as jnp
@@ -6,6 +7,22 @@
 
 N_SLOPES = 112
 epsilon = 1e-05
+
+
+def _serve_table(my_data, ax_name, axis_k):
+    heard = jnp.concatenate(
+        lax.all_to_all(
+            jnp.stack([my_data] * lax.axis_size(ax_name), axis=0),
+            axis_name=ax_name,
+            split_axis=0,
+            concat_axis=0,
+        ),
+        axis=axis_k,
+    )
+    return heard
+
+
+extend_the_teams = functools.partial(_serve_table, ax_name="tp", axis_k=1)
 
 
 def slope_values(slope_index):
@@ -53,7 +70,7 @@
         "hst,tha->sha", attention, values, preferred_element_type=jnp.float32
     ).astype(jnp.bfloat16)
     context = context.reshape(seq_rows, heads_here * head_size)
-    everything = lax.all_gather(context, "tp", axis=1, tiled=True)
+    everything = extend_the_teams(context)
     groups = lax.axis_size("tp")
     group_width = heads_here * head_size
     context_blocks = everything.reshape(seq_rows, groups, group_width)

time: 401 us -> 433 us (1.080); the launches traced: 400 us -> 427 us
  waiting for transfers between devices: 233 us -> 253 us
  starting transfers between devices: 0.04 us -> 5.84 us
    all_to_all x0 -> x1, waiting for transfers between devices: none -> 44.7 us  [_serve_table(): lax.all_to_all(jnp.stack([my_data] * lax.axis_size(ax_name), axis=0), axi...]
    all_gather x1 -> x0, waiting for transfers between devices: 25 us -> none  [shards(): everything = lax.all_gather(context, 'tp', axis=1, tiled=True)]
    all_to_all x0 -> x1, starting transfers between devices: none -> 5.84 us  [_serve_table(): lax.all_to_all(jnp.stack([my_data] * lax.axis_size(ax_name), axis=0), axi...]
  transfers between devices with their start and end apart: 2 -> 2, of which waited for: 2 -> 2; matrix products, arithmetic and copies ran while one was open for 8% -> 7% of each run, Pallas kernels for 0% -> 0%
where the time goes in v1:
time: 433 us; the launch traced here: 427 us
  waiting for transfers between devices  253 us (58%)
  local copies, waits for them, and re-layouts  45.8 us (11%)
  blocking collectives  41.7 us (10%)
  matrix products  39.7 us (9%)
  other arithmetic  27.6 us (6%)
  between operations  13.5 us (3%)
  starting transfers between devices  5.84 us (1%)
    all_gather x1, waiting for transfers between devices, shards(): weight_piece = lax.all_gather(regrouped, 'rep', axis=0, tiled=True)  208 us
    all_to_all x1, waiting for transfers between devices, _serve_table(): lax.all_to_all(jnp.stack([my_data] * lax.axis_size(ax_name), axis=0), axi...  44.7 us
    all_to_all x1, blocking collectives, shards(): lax.all_to_all(qkv_weight, 'tp', split_axis=1, concat_axis=0, tiled=True)  41.7 us
    all_gather x1, local copies, waits for them, and re-layouts, shards(): weight_piece = lax.all_gather(regrouped, 'rep', axis=0, tiled=True)  26.1 us
    dot_general x1, matrix products, shards(): projected = jnp.dot(normed, flat_piece, preferred_element_type=jnp.float32)  18 us
    dot_general x1, matrix products, shards(): jnp.einsum('sgk,dgk->gsd', context_blocks, weight_blocks, preferred_eleme...  17.5 us
    reduce_sum x1, other arithmetic, layer_norm(): variance = jnp.mean(centred * centred, axis=-1, keepdims=True)  11.6 us
    reshape x1, local copies, waits for them, and re-layouts, shards(): weight_blocks = out_weight.reshape(out_weight.shape[0], groups, group_width)  11.5 us
  transfers between devices with their start and end apart: 2, of which 2 were waited for; matrix products, arithmetic and copies ran while one was open for 7% of the time, Pallas kernels for 0%

profile of v1, /device:TPU:1, one launch (start us, length us, event | category | flops | bytes accessed | tf_op | source)
XLA Modules:
  0.0 427.4 jit_solution(4483350790455405103)
XLA Ops:
  6.5 2.8 copy.17
  9.3 41.7 %all_to_all.23 = bf16[112,32,384]{2,0,1:T(8,128)(2,1)S(1)} all-to-all(bf16[112,32,384]{2,0,1:T(8,128)(2,1)S(1)} %copy.17), channel_id=1, replica_groups=mesh['rep'=8,'tp'=16] {'tp'}, dimensions={1} | all-to-all | bytes 5505024 | tf_op jit(solution)/shard_map/all_to_all | solution.py:50
  51.0 1.8 copy.18
  52.8 0.0 all-gather.2.cloned.1.call-update
  52.9 0.2 broadcast_compare_fusion
  53.1 0.1 subtract_convert_fusion
  53.2 0.3 copy-done.5
  53.5 7.2 %convert_reduce_fusion = f32[512]{0:T(512)S(1)} fusion(bf16[512,14336]{1,0:T(8,128)(2,1)} %param.8), kind=kLoop, calls=%fused_computation.2 | loop fusion | flops 14679552 | bytes 14682112 | tf_op jit(solution)/shard_map/reduce_sum | solution.py:38
  60.7 11.6 %fusion.3 = f32[512]{0:T(512)S(1)} fusion(bf16[512,14336]{1,0:T(8,128)(2,1)} %param.8, f32[512]{0:T(512)S(1)} %broadcast_multiply_fusion), kind=kLoop, calls=%fused_computation.5 | loop fusion | flops 29359616 | bytes 14684160 | tf_op jit(solution)/shard_map/reduce_sum | solution.py:40
  72.3 208.5 %all-gather.2.cloned.1.call-done = bf16[14336,2,384]{2,0,1:T(8,128)(2,1)} async-done(((bf16[1792,2,384]{2,0,1:T(8,128)(2,1)}), bf16[14336,2,384]{2,0,1:T(8,128)(2,1)}) %all-gather.2.cloned.1.call-update) | async-done | bytes 22020112 | tf_op jit(solution)/shard_map/all_gather | solution.py:51
  280.8 26.1 %copy.19 = bf16[14336,2,384]{0,2,1:T(8,128)(2,1)} copy(bf16[14336,2,384]{2,0,1:T(8,128)(2,1)} %all-gather.2.cloned.1.call-done) | data formatting | bytes 44040192 | tf_op jit(solution)/shard_map/all_gather | solution.py:51
  306.9 18.0 %add_convert_fusion.1 = bf16[512,2,384]{2,0,1:T(8,128)(2,1)S(1)} fusion(bf16[14336,2,384]{0,2,1:T(8,128)(2,1)} %copy.19, bf16[512,14336]{1,0:T(8,128)(2,1)} %param.8, f32[14336]{0:T(1024)S(1)} %copy-done.2, f32[14336]{0:T(1024)S(1)} %copy-done.3, f32[512]{0:T(512)S(1)} %add_rsqrt_fusion, f32[512]{0:T(512)S(1)} %broadcast_multiply_fusion, ...), kind=kOutput, calls=%fused_computation.24 | convolution fusion | flops 11319115776 | bytes 37608448 | tf_op jit(solution)/shard_map/dot_general | solution.py:53
  324.9 0.9 copy-done
  325.8 0.6 subtract_select_fusion
  326.4 2.1 fusion.31
  328.4 1.6 convolution_convert_fusion.1
  330.0 0.1 copy.22
  330.2 2.3 stack.3
  332.5 5.8 %all-to-all-start.1 = ((bf16[16,512,256]{2,1,0:T(8,128)(2,1)}), bf16[16,512,256]{2,1,0:T(8,128)(2,1)}, u32[]{:S(2)}, u32[]{:S(2)}) async-start(bf16[16,512,256]{2,1,0:T(8,128)(2,1)} %stack.3), calls=%async_computation.1 | async-start | bytes 8388608 | tf_op jit(solution)/shard_map/all_to_all | solution.py:14
  338.3 11.5 %reshape.47 = bf16[896,16,256]{2,1,0:T(8,128)(2,1)} reshape(bf16[896,32,128]{2,1,0:T(8,128)(2,1)} %param.13) | data formatting | bytes 14680064 | tf_op jit(solution)/shard_map/reshape | solution.py:77
  349.8 44.7 %all-to-all-done.1 = bf16[16,512,256]{2,1,0:T(8,128)(2,1)} async-done(((bf16[16,512,256]{2,1,0:T(8,128)(2,1)}), bf16[16,512,256]{2,1,0:T(8,128)(2,1)}, u32[]{:S(2)}, u32[]{:S(2)}) %all-to-all-start.1) | async-done | bytes 4194336 | tf_op jit(solution)/shard_map/all_to_all | solution.py:14
  394.6 17.5 %convolution_convert_fusion = bf16[16,512,896]{2,1,0:T(8,128)(2,1)} fusion(bf16[896,16,256]{2,1,0:T(8,128)(2,1)} %reshape.47, bf16[16,512,256]{2,1,0:T(8,128)(2,1)} %all-to-all-done.1), kind=kOutput, calls=%fused_computation.17 | convolution fusion | flops 3765436416 | bytes 26214400 | tf_op jit(solution)/shard_map/sgk,dgk->gsd/dot_general | solution.py:78
  412.1 7.4 %convert_reduce_fusion.1 = f32[512,896]{1,0:T(8,128)S(1)} fusion(bf16[16,512,896]{2,1,0:T(8,128)(2,1)} %convolution_convert_fusion), kind=kLoop, calls=%fused_computation.9 | loop fusion | flops 14221312 | bytes 16515072 | tf_op jit(solution)/shard_map/reduce_sum | solution.py:82
  419.5 1.0 add_convert_fusion
  (14 shorter events, 0.1 us)
Async XLA Ops:
  6.5 274.3 %all-gather.2.cloned.1.call-start = ((), (), s32[]{:S(2)}) async-start(), calls=%async_computation.2 | async-start | bytes 24772608 | tf_op jit(solution)/shard_map/all_gather | solution.py:51
  52.8 0.7 copy-start.5
  72.3 234.6 %copy-start.2 = (f32[14336]{0:T(1024)S(1)}, f32[14336]{0:T(1024)}, u32[]{:S(2)}) copy-start(f32[14336]{0:T(1024)} %param.10) | copy-start | bytes 172036
  72.3 234.6 %copy-start.3 = (f32[14336]{0:T(1024)S(1)}, f32[14336]{0:T(1024)}, u32[]{:S(2)}) copy-start(f32[14336]{0:T(1024)} %param.9) | copy-start | bytes 172036
  72.3 234.6 %copy-start.4 = (f32[2,384]{1,0:T(2,128)S(1)}, f32[2,384]{1,0:T(2,128)}, u32[]{:S(2)}) copy-start(f32[2,384]{1,0:T(2,128)} %param.12) | copy-start | bytes 9220
  324.9 0.9 copy-start
  332.5 62.0 %all-to-all-start.1 = ((bf16[16,512,256]{2,1,0:T(8,128)(2,1)}), bf16[16,512,256]{2,1,0:T(8,128)(2,1)}, u32[]{:S(2)}, u32[]{:S(2)}) async-start(bf16[16,512,256]{2,1,0:T(8,128)(2,1)} %stack.3), calls=%async_computation.1 | async-start | bytes 8388608 | tf_op jit(solution)/shard_map/all_to_all | solution.py:14
  412.1 7.4 %copy-start.1 = (f32[896]{0:T(1024)S(1)}, f32[896]{0:T(1024)}, u32[]{:S(2)}) copy-start(f32[896]{0:T(1024)} %param.14) | copy-start | bytes 10756
Sparse Core Ops, SparseCore 0:
  53.0 227.7 all-gather.1
